TPU v7x, 32 devices: a whole 2x2x4 slice. The times are simulated.
32 devices in a mesh: grp: 2 (over y), row: 16 (over z, x, core).
Axes of the slice: x: 2, y: 2, z: 4, core: 2. Of those that a mesh axis runs over, the one named last changes fastest.
Arguments:
- right_side: float32 [64, 4096], P(None, ('grp', 'row')), may hold values from -60 to 60
- links: int32 [8, 4096], P(None, ('grp', 'row')), may hold values from 0 to 4095, as said below
- coefs: float32 [4096], P(('grp', 'row')), may hold values from 0.3 to 3
- reaction: float32 [4096], P(('grp', 'row')), may hold values from 0.05 to 0.5
Outputs:
- solution: float32 [64, 4096], P(None, ('grp', 'row'))
- resid_rms: float32 [2, 64], replicated
Inputs may be any that keep to these rules, and one draw needn't show every extreme that they name: `links`: the nodes form a periodic grid of 8 x 32 x 16. Block (p, q), p < 2, q < 16, holds the nodes of first coordinate p * 4 to p * 4 + 3 and second coordinate q * 2 to q * 2 + 1, and these carry the unknowns and elements b * 4 * 2 * 16 to (b + 1) * 4 * 2 * 16 - 1, with b = p * 16 + q. Element b * 4 * 2 * 16 + (i * 2 + j) * 16 + k has its base at the node (p * 4 + i, q * 2 + j, k), and its corner l lies at the base plus (l mod 2, l // 2 mod 2, l // 4), modulo the grid. Within a block the unknowns are numbered in some order. Every unknown is a corner of 8 elements.
All inputs are finite; a program needn't handle non-finite values.
Results may differ from a plain program's by a relative error of at most 0.0003.
Values sent between devices are 32-bit elements; how exact they have to be, the bound alone decides.
A program may use at most 64 MiB of HBM per device.

v0:
```python
import math

import jax
import jax.numpy as jnp
import numpy as np
from jax import lax
from jax.sharding import PartitionSpec as P

SWEEPS = 2
DEGREE = 4


def shifted(block, axis, distance):
    devices = range(lax.axis_size(axis))
    route = [((i - distance) % len(devices), i) for i in devices]
    return lax.ppermute(block, axis, route)


def element_matrix():
    node_ids = np.arange(8)
    corner = np.stack([node_ids % 2, node_ids // 2 % 2, node_ids // 4], axis=1)
    gauss_points = np.array([0.5 - 0.5 / math.sqrt(3.0), 0.5 + 0.5 / math.sqrt(3.0)])
    stiffness = np.zeros((8, 8))
    for q in range(8):
        quad_point = gauss_points[np.array([q % 2, q // 2 % 2, q // 4])]
        values = np.where(corner > 0.5, quad_point, 1.0 - quad_point)
        slopes = np.where(corner > 0.5, 1.0, -1.0)
        gradient = np.stack(
            [
                slopes[:, 0] * values[:, 1] * values[:, 2],
                values[:, 0] * slopes[:, 1] * values[:, 2],
                values[:, 0] * values[:, 1] * slopes[:, 2],
            ],
            axis=1,
        )
        stiffness = stiffness + gradient @ gradient.T / 8.0
    return stiffness


def element_images(window, offsets, weights, stiffness):
    corners = window[:, offsets]
    images = (
        jnp.einsum("ml,rle->rme", stiffness, corners, precision=lax.Precision.HIGHEST) * weights
    )
    return jnp.zeros_like(window).at[:, offsets].add(images)


def on_device(right_side, links, coefs, reaction):
    stiffness = jnp.asarray(element_matrix(), dtype=jnp.float32)
    count = right_side.shape[1]
    groups = lax.axis_size("grp")
    rowcount = lax.axis_size("row")
    group_id = lax.axis_index("grp")
    row_id = lax.axis_index("row")
    total = count * groups * rowcount
    owner = links // count
    slot = links % count
    first = jnp.mod(owner // rowcount - group_id, groups)
    second = jnp.mod(owner % rowcount - row_id, rowcount)
    offsets = (first * 2 + second) * count + slot

    def apply_operator(field):
        above_row = shifted(field, "row", -1)
        upper = shifted(jnp.stack([field, above_row], axis=0), "grp", -1)
        window = jnp.concatenate([field, above_row, upper[0], upper[1]], axis=1)
        summed = element_images(window, offsets, coefs, stiffness)
        back = shifted(
            jnp.stack([summed[:, 2 * count : 3 * count], summed[:, 3 * count :]], axis=0), "grp", 1
        )
        first_col = summed[:, :count] + back[0]
        second_col = summed[:, count : 2 * count] + back[1]
        first_col = first_col + shifted(second_col, "row", 1)
        return first_col + reaction * field

    image = apply_operator(right_side)
    cross, square = lax.psum(
        (jnp.sum(right_side * image, axis=1), jnp.sum(image * image, axis=1)), ("grp", "row")
    )
    theta = square / cross
    upper = (1.5 * theta)[:, None]
    lower = upper / 10.0
    center = (upper + lower) / 2.0
    half = (upper - lower) / 2.0
    sigma = center / half
    solution = jnp.zeros_like(right_side)
    residual = right_side
    history = []
    for sweep in range(SWEEPS):
        start = residual
        correction = jnp.zeros_like(right_side)
        rho_now = 1.0 / sigma
        direction = residual / center
        for step in range(DEGREE):
            correction = correction + direction
            residual = residual - apply_operator(direction)
            if step + 1 < DEGREE:
                rho_next = 1.0 / (2.0 * sigma - rho_now)
                direction = rho_next * rho_now * direction + 2.0 * rho_next / half * residual
                rho_now = rho_next
        change = start - residual
        along, length, begin = lax.psum(
            (
                jnp.sum(start * change, axis=1),
                jnp.sum(change * change, axis=1),
                jnp.sum(start * start, axis=1),
            ),
            ("grp", "row"),
        )
        omega = along / length
        residual = start - omega[:, None] * change
        squares = begin - 2.0 * omega * along + omega * omega * length
        solution = solution + omega[:, None] * correction
        history.append(jnp.sqrt(squares / total))
    return (solution, jnp.stack(history, axis=0))


def solution(mesh):
    return jax.shard_map(
        on_device,
        mesh=mesh,
        in_specs=(
            P(None, ("grp", "row")),
            P(None, ("grp", "row")),
            P(("grp", "row")),
            P(("grp", "row")),
        ),
        out_specs=(P(None, ("grp", "row")), P()),
        check_vma=False,
    )
```

profile of v0, /device:TPU:0, one launch (start us, length us, event | category | flops | bytes accessed | tf_op | source)
XLA Modules:
  0.0 381.8 jit_solution(4145914351911960971)
XLA Ops:
  1.5 5.5 %collective-permute-start = (f32[64,128]{0,1:T(8,128)S(1)}, f32[64,128]{0,1:T(8,128)S(1)}, u32[]{:S(2)}, u32[]{:S(2)}) collective-permute-start(f32[64,128]{0,1:T(8,128)S(1)} %copy.25), channel_id=1, source_target_pairs={{1,0},{2,1},{3,2},{4,3},{5,4},{6,5},{7,6},{8,7},{9,8},{10,9},{11,1... | collective-permute-start | bytes 98312 | tf_op jit(solution)/shard_map/ppermute | solution.py:16
  18.1 6.1 %scatter_custom_fusion = f32[64,512]{0,1:T(8,128)S(1)} fusion(s32[1024]{0:T(1024)S(1)} %get-tuple-element.40, f32[1024,64]{1,0:T(8,128)S(1)} %bitcast.332, f32[]{:T(128)} %constant.79.clone.1), kind=kCustom, calls=%fused_computation.88 | custom fusion | flops 65536 | bytes 131076 | tf_op jit(solution)/shard_map/scatter-add | solution.py:45
  25.8 3.4 collective-permute-done.2
  29.3 6.4 %collective-permute-done.3 = f32[64,128]{0,1:T(8,128)S(1)} collective-permute-done((f32[64,128]{0,1:T(8,128)S(1)}, f32[64,128]{0,1:T(8,128)S(1)}, u32[]{:S(2)}, u32[]{:S(2)}) %collective-permute-start.3) | collective-permute-done | bytes 32800 | tf_op jit(solution)/shard_map/ppermute | solution.py:16
  35.8 36.8 %all-reduce.2 = (f32[64]{0:T(128)S(1)}, f32[64]{0:T(128)S(1)}) all-reduce(f32[64]{0:T(128)S(1)} %get-tuple-element.10, f32[64]{0:T(128)S(1)} %get-tuple-element.9), channel_id=1, replica_groups=mesh['grp'=2,'row'=16] {'grp','row'}, use_global_device_ids=true, to_apply=%region_2.3 | all-reduce | flops 128 | bytes 1024 | tf_op jit(solution)/shard_map/psum | solution.py:76
  77.9 4.7 %collective-permute-done.5 = f32[2,64,128]{1,2,0:T(8,128)S(1)} collective-permute-done((f32[2,64,128]{1,2,0:T(8,128)S(1)}, f32[2,64,128]{1,2,0:T(8,128)S(1)}, u32[]{:S(2)}, u32[]{:S(2)}) %collective-permute-start.5) | collective-permute-done | bytes 65568 | tf_op jit(solution)/shard_map/ppermute | solution.py:16
  86.2 6.1 %scatter_custom_fusion.1 = f32[64,512]{0,1:T(8,128)S(1)} fusion(s32[1024]{0:T(1024)S(1)} %get-tuple-element.40, f32[1024,64]{1,0:T(8,128)S(1)} %bitcast.333, f32[]{:T(128)} %constant.79.clone.1), kind=kCustom, calls=%fused_computation.86 | custom fusion | flops 65536 | bytes 131076 | tf_op jit(solution)/shard_map/scatter-add | solution.py:45
  94.0 3.6 collective-permute-done.6
  97.6 6.5 %collective-permute-done.7 = f32[64,128]{0,1:T(8,128)S(1)} collective-permute-done((f32[64,128]{0,1:T(8,128)S(1)}, f32[64,128]{0,1:T(8,128)S(1)}, u32[]{:S(2)}, u32[]{:S(2)}) %collective-permute-start.7) | collective-permute-done | bytes 32800 | tf_op jit(solution)/shard_map/ppermute | solution.py:16
  107.9 3.3 collective-permute-done.9
  114.8 6.1 %scatter_custom_fusion.2 = f32[64,512]{0,1:T(8,128)S(1)} fusion(s32[1024]{0:T(1024)S(1)} %get-tuple-element.40, f32[1024,64]{1,0:T(8,128)S(1)} %bitcast.334, f32[]{:T(128)} %constant.79.clone.1), kind=kCustom, calls=%fused_computation.84 | custom fusion | flops 65536 | bytes 131076 | tf_op jit(solution)/shard_map/scatter-add | solution.py:45
  122.7 3.3 collective-permute-done.10
  126.1 6.4 %collective-permute-done.11 = f32[64,128]{0,1:T(8,128)S(1)} collective-permute-done((f32[64,128]{0,1:T(8,128)S(1)}, f32[64,128]{0,1:T(8,128)S(1)}, u32[]{:S(2)}, u32[]{:S(2)}) %collective-permute-start.11) | collective-permute-done | bytes 32800 | tf_op jit(solution)/shard_map/ppermute | solution.py:16
  136.5 3.3 collective-permute-done.13
  143.4 6.1 %scatter_custom_fusion.3 = f32[64,512]{0,1:T(8,128)S(1)} fusion(s32[1024]{0:T(1024)S(1)} %get-tuple-element.40, f32[1024,64]{1,0:T(8,128)S(1)} %bitcast.335, f32[]{:T(128)} %constant.79.clone.1), kind=kCustom, calls=%fused_computation.82 | custom fusion | flops 65536 | bytes 131076 | tf_op jit(solution)/shard_map/scatter-add | solution.py:45
  151.3 3.3 collective-permute-done.14
  154.6 6.4 %collective-permute-done.15 = f32[64,128]{0,1:T(8,128)S(1)} collective-permute-done((f32[64,128]{0,1:T(8,128)S(1)}, f32[64,128]{0,1:T(8,128)S(1)}, u32[]{:S(2)}, u32[]{:S(2)}) %collective-permute-start.15) | collective-permute-done | bytes 32800 | tf_op jit(solution)/shard_map/ppermute | solution.py:16
  164.8 3.3 collective-permute-done.17
  171.8 6.1 %scatter_custom_fusion.4 = f32[64,512]{0,1:T(8,128)S(1)} fusion(s32[1024]{0:T(1024)S(1)} %get-tuple-element.40, f32[1024,64]{1,0:T(8,128)S(1)} %bitcast.336, f32[]{:T(128)} %constant.79.clone.1), kind=kCustom, calls=%fused_computation.80 | custom fusion | flops 65536 | bytes 131076 | tf_op jit(solution)/shard_map/scatter-add | solution.py:45
  183.0 6.4 %collective-permute-done.19 = f32[64,128]{0,1:T(8,128)S(1)} collective-permute-done((f32[64,128]{0,1:T(8,128)S(1)}, f32[64,128]{0,1:T(8,128)S(1)}, u32[]{:S(2)}, u32[]{:S(2)}) %collective-permute-start.19) | collective-permute-done | bytes 32800 | tf_op jit(solution)/shard_map/ppermute | solution.py:16
  189.5 36.9 %all-reduce.1 = (f32[64]{0:T(128)S(1)}, f32[64]{0:T(128)S(1)}) all-reduce(f32[64]{0:T(128)S(1)} %get-tuple-element.8, f32[64]{0:T(128)S(1)} %get-tuple-element.7), channel_id=1, replica_groups=mesh['grp'=2,'row'=16] {'grp','row'}, use_global_device_ids=true, to_apply=%region_10.11 | all-reduce | flops 128 | bytes 1024 | tf_op jit(solution)/shard_map/psum | solution.py:101
  231.7 4.6 %collective-permute-done.21 = f32[2,64,128]{1,2,0:T(8,128)S(1)} collective-permute-done((f32[2,64,128]{1,2,0:T(8,128)S(1)}, f32[2,64,128]{1,2,0:T(8,128)S(1)}, u32[]{:S(2)}, u32[]{:S(2)}) %collective-permute-start.21) | collective-permute-done | bytes 65568 | tf_op jit(solution)/shard_map/ppermute | solution.py:16
  240.0 6.1 %scatter_custom_fusion.5 = f32[64,512]{0,1:T(8,128)S(1)} fusion(s32[1024]{0:T(1024)S(1)} %get-tuple-element.40, f32[1024,64]{1,0:T(8,128)S(1)} %bitcast.337, f32[]{:T(128)} %constant.79.clone.1), kind=kCustom, calls=%fused_computation.78 | custom fusion | flops 65536 | bytes 131076 | tf_op jit(solution)/shard_map/scatter-add | solution.py:45
  247.8 3.7 collective-permute-done.22
  251.5 6.5 %collective-permute-done.23 = f32[64,128]{0,1:T(8,128)S(1)} collective-permute-done((f32[64,128]{0,1:T(8,128)S(1)}, f32[64,128]{0,1:T(8,128)S(1)}, u32[]{:S(2)}, u32[]{:S(2)}) %collective-permute-start.23) | collective-permute-done | bytes 32800 | tf_op jit(solution)/shard_map/ppermute | solution.py:16
  269.0 6.1 %scatter_custom_fusion.6 = f32[64,512]{0,1:T(8,128)S(1)} fusion(s32[1024]{0:T(1024)S(1)} %get-tuple-element.40, f32[1024,64]{1,0:T(8,128)S(1)} %bitcast.338, f32[]{:T(128)} %constant.79.clone.1), kind=kCustom, calls=%fused_computation.76 | custom fusion | flops 65536 | bytes 131076 | tf_op jit(solution)/shard_map/scatter-add | solution.py:45
  280.2 6.4 %collective-permute-done.27 = f32[64,128]{0,1:T(8,128)S(1)} collective-permute-done((f32[64,128]{0,1:T(8,128)S(1)}, f32[64,128]{0,1:T(8,128)S(1)}, u32[]{:S(2)}, u32[]{:S(2)}) %collective-permute-start.27) | collective-permute-done | bytes 32800 | tf_op jit(solution)/shard_map/ppermute | solution.py:16
  297.4 6.1 %scatter_custom_fusion.7 = f32[64,512]{0,1:T(8,128)S(1)} fusion(s32[1024]{0:T(1024)S(1)} %get-tuple-element.40, f32[1024,64]{1,0:T(8,128)S(1)} %bitcast.339, f32[]{:T(128)} %constant.79.clone.1), kind=kCustom, calls=%fused_computation.74 | custom fusion | flops 65536 | bytes 131076 | tf_op jit(solution)/shard_map/scatter-add | solution.py:45
  308.6 6.4 %collective-permute-done.31 = f32[64,128]{0,1:T(8,128)S(1)} collective-permute-done((f32[64,128]{0,1:T(8,128)S(1)}, f32[64,128]{0,1:T(8,128)S(1)}, u32[]{:S(2)}, u32[]{:S(2)}) %collective-permute-start.31) | collective-permute-done | bytes 32800 | tf_op jit(solution)/shard_map/ppermute | solution.py:16
  325.8 6.1 %scatter_custom_fusion.8 = f32[64,512]{0,1:T(8,128)S(1)} fusion(s32[1024]{0:T(1024)S(1)} %get-tuple-element.40, f32[1024,64]{1,0:T(8,128)S(1)} %bitcast.331, f32[]{:T(128)} %constant.79.clone.1), kind=kCustom, calls=%fused_computation.72 | custom fusion | flops 65536 | bytes 131076 | tf_op jit(solution)/shard_map/scatter-add | solution.py:45
  337.1 6.3 %collective-permute-done.35 = f32[64,128]{0,1:T(8,128)S(1)} collective-permute-done((f32[64,128]{0,1:T(8,128)S(1)}, f32[64,128]{0,1:T(8,128)S(1)}, u32[]{:S(2)}, u32[]{:S(2)}) %collective-permute-start.35) | collective-permute-done | bytes 32800 | tf_op jit(solution)/shard_map/ppermute | solution.py:16
  343.5 36.9 %all-reduce = (f32[64]{0:T(128)S(1)}, f32[64]{0:T(128)S(1)}, f32[64]{0:T(128)S(1)}, f32[64]{0:T(128)S(1)}) all-reduce(f32[64]{0:T(128)S(1)} %get-tuple-element.5, f32[64]{0:T(128)S(1)} %get-tuple-element.6, f32[64]{0:T(128)S(1)} %get-tuple-element.4, f32[64]{0:T(128)S(1)} %multiply_reduce_fusion.7), channel_id=1, replica_groups=mesh['grp'=2,'row'=16] {'grp','row'}, use_global_device_ids=true, to_apply=%region_18.19 | all-reduce | flops 256 | bytes 2048 | tf_op jit(solution)/shard_map/psum | solution.py:101
  (174 shorter events, 115.4 us)
Async XLA Ops:
  1.5 7.4 %collective-permute-start = (f32[64,128]{0,1:T(8,128)S(1)}, f32[64,128]{0,1:T(8,128)S(1)}, u32[]{:S(2)}, u32[]{:S(2)}) collective-permute-start(f32[64,128]{0,1:T(8,128)S(1)} %copy.25), channel_id=1, source_target_pairs={{1,0},{2,1},{3,2},{4,3},{5,4},{6,5},{7,6},{8,7},{9,8},{10,9},{11,1... | collective-permute-start | bytes 98312 | tf_op jit(solution)/shard_map/ppermute | solution.py:16
  8.9 5.0 %collective-permute-start.1 = (f32[2,64,128]{1,2,0:T(8,128)S(1)}, f32[2,64,128]{1,2,0:T(8,128)S(1)}, u32[]{:S(2)}, u32[]{:S(2)}) collective-permute-start(f32[2,64,128]{1,2,0:T(8,128)S(1)} %pad_maximum_fusion.9), channel_id=1, source_target_pairs={{16,0},{0,16},{17,1},{1,17},{18,2},{2,18},{19,3},{3,19},{20,4},{4,... | collective-permute-start | bytes 196616 | tf_op jit(solution)/shard_map/ppermute | solution.py:16
  24.2 5.0 %collective-permute-start.2 = (f32[2,64,128]{1,2,0:T(8,128)S(1)}, f32[2,64,128]{1,2,0:T(8,128)S(1)}, u32[]{:S(2)}, u32[]{:S(2)}) collective-permute-start(f32[2,64,128]{1,2,0:T(8,128)S(1)} %pad_maximum_fusion.10), channel_id=1, source_target_pairs={{16,0},{0,16},{17,1},{1,17},{18,2},{2,18},{19,3},{3,19},{20,4},{4,... | collective-permute-start | bytes 196616 | tf_op jit(solution)/shard_map/ppermute | solution.py:16
  29.3 6.4 %collective-permute-start.3 = (f32[64,128]{0,1:T(8,128)S(1)}, f32[64,128]{0,1:T(8,128)S(1)}, u32[]{:S(2)}, u32[]{:S(2)}) collective-permute-start(f32[64,128]{0,1:T(8,128)S(1)} %fusion.78), channel_id=1, source_target_pairs={{15,0},{0,1},{1,2},{2,3},{3,4},{4,5},{5,6},{6,7},{7,8},{8,9},{9,10... | collective-permute-start | bytes 98312 | tf_op jit(solution)/shard_map/ppermute | solution.py:16
  72.7 4.6 %collective-permute-start.4 = (f32[64,128]{0,1:T(8,128)S(1)}, f32[64,128]{0,1:T(8,128)S(1)}, u32[]{:S(2)}, u32[]{:S(2)}) collective-permute-start(f32[64,128]{0,1:T(8,128)S(1)} %get-tuple-element.78), channel_id=1, source_target_pairs={{1,0},{2,1},{3,2},{4,3},{5,4},{6,5},{7,6},{8,7},{9,8},{10,9},{11,1... | collective-permute-start | bytes 98312 | tf_op jit(solution)/shard_map/ppermute | solution.py:16
  77.3 5.2 %collective-permute-start.5 = (f32[2,64,128]{1,2,0:T(8,128)S(1)}, f32[2,64,128]{1,2,0:T(8,128)S(1)}, u32[]{:S(2)}, u32[]{:S(2)}) collective-permute-start(f32[2,64,128]{1,2,0:T(8,128)S(1)} %pad_maximum_fusion.11), channel_id=1, source_target_pairs={{16,0},{0,16},{17,1},{1,17},{18,2},{2,18},{19,3},{3,19},{20,4},{4,... | collective-permute-start | bytes 196616 | tf_op jit(solution)/shard_map/ppermute | solution.py:16
  92.3 5.2 %collective-permute-start.6 = (f32[2,64,128]{1,2,0:T(8,128)S(1)}, f32[2,64,128]{1,2,0:T(8,128)S(1)}, u32[]{:S(2)}, u32[]{:S(2)}) collective-permute-start(f32[2,64,128]{1,2,0:T(8,128)S(1)} %pad_maximum_fusion.12), channel_id=1, source_target_pairs={{16,0},{0,16},{17,1},{1,17},{18,2},{2,18},{19,3},{3,19},{20,4},{4,... | collective-permute-start | bytes 196616 | tf_op jit(solution)/shard_map/ppermute | solution.py:16
  97.5 6.5 %collective-permute-start.7 = (f32[64,128]{0,1:T(8,128)S(1)}, f32[64,128]{0,1:T(8,128)S(1)}, u32[]{:S(2)}, u32[]{:S(2)}) collective-permute-start(f32[64,128]{0,1:T(8,128)S(1)} %fusion.73), channel_id=1, source_target_pairs={{15,0},{0,1},{1,2},{2,3},{3,4},{4,5},{5,6},{6,7},{7,8},{8,9},{9,10... | collective-permute-start | bytes 98312 | tf_op jit(solution)/shard_map/ppermute | solution.py:16
  106.2 5.0 %collective-permute-start.9 = (f32[2,64,128]{1,2,0:T(8,128)S(1)}, f32[2,64,128]{1,2,0:T(8,128)S(1)}, u32[]{:S(2)}, u32[]{:S(2)}) collective-permute-start(f32[2,64,128]{1,2,0:T(8,128)S(1)} %pad_maximum_fusion.13), channel_id=1, source_target_pairs={{16,0},{0,16},{17,1},{1,17},{18,2},{2,18},{19,3},{3,19},{20,4},{4,... | collective-permute-start | bytes 196616 | tf_op jit(solution)/shard_map/ppermute | solution.py:16
  121.0 5.0 %collective-permute-start.10 = (f32[2,64,128]{1,2,0:T(8,128)S(1)}, f32[2,64,128]{1,2,0:T(8,128)S(1)}, u32[]{:S(2)}, u32[]{:S(2)}) collective-permute-start(f32[2,64,128]{1,2,0:T(8,128)S(1)} %pad_maximum_fusion.14), channel_id=1, source_target_pairs={{16,0},{0,16},{17,1},{1,17},{18,2},{2,18},{19,3},{3,19},{20,4},{4,... | collective-permute-start | bytes 196616 | tf_op jit(solution)/shard_map/ppermute | solution.py:16
  126.0 6.4 %collective-permute-start.11 = (f32[64,128]{0,1:T(8,128)S(1)}, f32[64,128]{0,1:T(8,128)S(1)}, u32[]{:S(2)}, u32[]{:S(2)}) collective-permute-start(f32[64,128]{0,1:T(8,128)S(1)} %fusion.68), channel_id=1, source_target_pairs={{15,0},{0,1},{1,2},{2,3},{3,4},{4,5},{5,6},{6,7},{7,8},{8,9},{9,10... | collective-permute-start | bytes 98312 | tf_op jit(solution)/shard_map/ppermute | solution.py:16
  132.6 2.1 collective-permute-start.12
  134.7 5.0 %collective-permute-start.13 = (f32[2,64,128]{1,2,0:T(8,128)S(1)}, f32[2,64,128]{1,2,0:T(8,128)S(1)}, u32[]{:S(2)}, u32[]{:S(2)}) collective-permute-start(f32[2,64,128]{1,2,0:T(8,128)S(1)} %pad_maximum_fusion.15), channel_id=1, source_target_pairs={{16,0},{0,16},{17,1},{1,17},{18,2},{2,18},{19,3},{3,19},{20,4},{4,... | collective-permute-start | bytes 196616 | tf_op jit(solution)/shard_map/ppermute | solution.py:16
  149.5 5.0 %collective-permute-start.14 = (f32[2,64,128]{1,2,0:T(8,128)S(1)}, f32[2,64,128]{1,2,0:T(8,128)S(1)}, u32[]{:S(2)}, u32[]{:S(2)}) collective-permute-start(f32[2,64,128]{1,2,0:T(8,128)S(1)} %pad_maximum_fusion.16), channel_id=1, source_target_pairs={{16,0},{0,16},{17,1},{1,17},{18,2},{2,18},{19,3},{3,19},{20,4},{4,... | collective-permute-start | bytes 196616 | tf_op jit(solution)/shard_map/ppermute | solution.py:16
  154.6 6.4 %collective-permute-start.15 = (f32[64,128]{0,1:T(8,128)S(1)}, f32[64,128]{0,1:T(8,128)S(1)}, u32[]{:S(2)}, u32[]{:S(2)}) collective-permute-start(f32[64,128]{0,1:T(8,128)S(1)} %fusion.63), channel_id=1, source_target_pairs={{15,0},{0,1},{1,2},{2,3},{3,4},{4,5},{5,6},{6,7},{7,8},{8,9},{9,10... | collective-permute-start | bytes 98312 | tf_op jit(solution)/shard_map/ppermute | solution.py:16
  163.1 5.0 %collective-permute-start.17 = (f32[2,64,128]{1,2,0:T(8,128)S(1)}, f32[2,64,128]{1,2,0:T(8,128)S(1)}, u32[]{:S(2)}, u32[]{:S(2)}) collective-permute-start(f32[2,64,128]{1,2,0:T(8,128)S(1)} %pad_maximum_fusion.17), channel_id=1, source_target_pairs={{16,0},{0,16},{17,1},{1,17},{18,2},{2,18},{19,3},{3,19},{20,4},{4,... | collective-permute-start | bytes 196616 | tf_op jit(solution)/shard_map/ppermute | solution.py:16
  177.9 5.0 %collective-permute-start.18 = (f32[2,64,128]{1,2,0:T(8,128)S(1)}, f32[2,64,128]{1,2,0:T(8,128)S(1)}, u32[]{:S(2)}, u32[]{:S(2)}) collective-permute-start(f32[2,64,128]{1,2,0:T(8,128)S(1)} %pad_maximum_fusion.18), channel_id=1, source_target_pairs={{16,0},{0,16},{17,1},{1,17},{18,2},{2,18},{19,3},{3,19},{20,4},{4,... | collective-permute-start | bytes 196616 | tf_op jit(solution)/shard_map/ppermute | solution.py:16
  182.9 6.4 %collective-permute-start.19 = (f32[64,128]{0,1:T(8,128)S(1)}, f32[64,128]{0,1:T(8,128)S(1)}, u32[]{:S(2)}, u32[]{:S(2)}) collective-permute-start(f32[64,128]{0,1:T(8,128)S(1)} %fusion.57), channel_id=1, source_target_pairs={{15,0},{0,1},{1,2},{2,3},{3,4},{4,5},{5,6},{6,7},{7,8},{8,9},{9,10... | collective-permute-start | bytes 98312 | tf_op jit(solution)/shard_map/ppermute | solution.py:16
  226.5 4.7 %collective-permute-start.20 = (f32[64,128]{0,1:T(8,128)S(1)}, f32[64,128]{0,1:T(8,128)S(1)}, u32[]{:S(2)}, u32[]{:S(2)}) collective-permute-start(f32[64,128]{0,1:T(8,128)S(1)} %broadcast_divide_fusion), channel_id=1, source_target_pairs={{1,0},{2,1},{3,2},{4,3},{5,4},{6,5},{7,6},{8,7},{9,8},{10,9},{11,1... | collective-permute-start | bytes 98312 | tf_op jit(solution)/shard_map/ppermute | solution.py:16
  231.2 5.1 %collective-permute-start.21 = (f32[2,64,128]{1,2,0:T(8,128)S(1)}, f32[2,64,128]{1,2,0:T(8,128)S(1)}, u32[]{:S(2)}, u32[]{:S(2)}) collective-permute-start(f32[2,64,128]{1,2,0:T(8,128)S(1)} %pad_maximum_fusion.19), channel_id=1, source_target_pairs={{16,0},{0,16},{17,1},{1,17},{18,2},{2,18},{19,3},{3,19},{20,4},{4,... | collective-permute-start | bytes 196616 | tf_op jit(solution)/shard_map/ppermute | solution.py:16
  246.1 5.3 %collective-permute-start.22 = (f32[2,64,128]{1,2,0:T(8,128)S(1)}, f32[2,64,128]{1,2,0:T(8,128)S(1)}, u32[]{:S(2)}, u32[]{:S(2)}) collective-permute-start(f32[2,64,128]{1,2,0:T(8,128)S(1)} %pad_maximum_fusion.20), channel_id=1, source_target_pairs={{16,0},{0,16},{17,1},{1,17},{18,2},{2,18},{19,3},{3,19},{20,4},{4,... | collective-permute-start | bytes 196616 | tf_op jit(solution)/shard_map/ppermute | solution.py:16
  251.5 6.5 %collective-permute-start.23 = (f32[64,128]{0,1:T(8,128)S(1)}, f32[64,128]{0,1:T(8,128)S(1)}, u32[]{:S(2)}, u32[]{:S(2)}) collective-permute-start(f32[64,128]{0,1:T(8,128)S(1)} %fusion.52), channel_id=1, source_target_pairs={{15,0},{0,1},{1,2},{2,3},{3,4},{4,5},{5,6},{6,7},{7,8},{8,9},{9,10... | collective-permute-start | bytes 98312 | tf_op jit(solution)/shard_map/ppermute | solution.py:16
  258.1 2.2 collective-permute-start.24
  260.3 5.0 %collective-permute-start.25 = (f32[2,64,128]{1,2,0:T(8,128)S(1)}, f32[2,64,128]{1,2,0:T(8,128)S(1)}, u32[]{:S(2)}, u32[]{:S(2)}) collective-permute-start(f32[2,64,128]{1,2,0:T(8,128)S(1)} %pad_maximum_fusion.21), channel_id=1, source_target_pairs={{16,0},{0,16},{17,1},{1,17},{18,2},{2,18},{19,3},{3,19},{20,4},{4,... | collective-permute-start | bytes 196616 | tf_op jit(solution)/shard_map/ppermute | solution.py:16
  275.1 5.0 %collective-permute-start.26 = (f32[2,64,128]{1,2,0:T(8,128)S(1)}, f32[2,64,128]{1,2,0:T(8,128)S(1)}, u32[]{:S(2)}, u32[]{:S(2)}) collective-permute-start(f32[2,64,128]{1,2,0:T(8,128)S(1)} %pad_maximum_fusion.22), channel_id=1, source_target_pairs={{16,0},{0,16},{17,1},{1,17},{18,2},{2,18},{19,3},{3,19},{20,4},{4,... | collective-permute-start | bytes 196616 | tf_op jit(solution)/shard_map/ppermute | solution.py:16
  280.2 6.4 %collective-permute-start.27 = (f32[64,128]{0,1:T(8,128)S(1)}, f32[64,128]{0,1:T(8,128)S(1)}, u32[]{:S(2)}, u32[]{:S(2)}) collective-permute-start(f32[64,128]{0,1:T(8,128)S(1)} %fusion.47), channel_id=1, source_target_pairs={{15,0},{0,1},{1,2},{2,3},{3,4},{4,5},{5,6},{6,7},{7,8},{8,9},{9,10... | collective-permute-start | bytes 98312 | tf_op jit(solution)/shard_map/ppermute | solution.py:16
  288.7 5.0 %collective-permute-start.29 = (f32[2,64,128]{1,2,0:T(8,128)S(1)}, f32[2,64,128]{1,2,0:T(8,128)S(1)}, u32[]{:S(2)}, u32[]{:S(2)}) collective-permute-start(f32[2,64,128]{1,2,0:T(8,128)S(1)} %pad_maximum_fusion.23), channel_id=1, source_target_pairs={{16,0},{0,16},{17,1},{1,17},{18,2},{2,18},{19,3},{3,19},{20,4},{4,... | collective-permute-start | bytes 196616 | tf_op jit(solution)/shard_map/ppermute | solution.py:16
  303.5 5.0 %collective-permute-start.30 = (f32[2,64,128]{1,2,0:T(8,128)S(1)}, f32[2,64,128]{1,2,0:T(8,128)S(1)}, u32[]{:S(2)}, u32[]{:S(2)}) collective-permute-start(f32[2,64,128]{1,2,0:T(8,128)S(1)} %pad_maximum_fusion.24), channel_id=1, source_target_pairs={{16,0},{0,16},{17,1},{1,17},{18,2},{2,18},{19,3},{3,19},{20,4},{4,... | collective-permute-start | bytes 196616 | tf_op jit(solution)/shard_map/ppermute | solution.py:16
  308.6 6.4 %collective-permute-start.31 = (f32[64,128]{0,1:T(8,128)S(1)}, f32[64,128]{0,1:T(8,128)S(1)}, u32[]{:S(2)}, u32[]{:S(2)}) collective-permute-start(f32[64,128]{0,1:T(8,128)S(1)} %fusion.42), channel_id=1, source_target_pairs={{15,0},{0,1},{1,2},{2,3},{3,4},{4,5},{5,6},{6,7},{7,8},{8,9},{9,10... | collective-permute-start | bytes 98312 | tf_op jit(solution)/shard_map/ppermute | solution.py:16
  317.1 5.0 %collective-permute-start.33 = (f32[2,64,128]{1,2,0:T(8,128)S(1)}, f32[2,64,128]{1,2,0:T(8,128)S(1)}, u32[]{:S(2)}, u32[]{:S(2)}) collective-permute-start(f32[2,64,128]{1,2,0:T(8,128)S(1)} %pad_maximum_fusion.25), channel_id=1, source_target_pairs={{16,0},{0,16},{17,1},{1,17},{18,2},{2,18},{19,3},{3,19},{20,4},{4,... | collective-permute-start | bytes 196616 | tf_op jit(solution)/shard_map/ppermute | solution.py:16
  331.9 5.0 %collective-permute-start.34 = (f32[2,64,128]{1,2,0:T(8,128)S(1)}, f32[2,64,128]{1,2,0:T(8,128)S(1)}, u32[]{:S(2)}, u32[]{:S(2)}) collective-permute-start(f32[2,64,128]{1,2,0:T(8,128)S(1)} %pad_maximum_fusion.26), channel_id=1, source_target_pairs={{16,0},{0,16},{17,1},{1,17},{18,2},{2,18},{19,3},{3,19},{20,4},{4,... | collective-permute-start | bytes 196616 | tf_op jit(solution)/shard_map/ppermute | solution.py:16
  337.0 6.4 %collective-permute-start.35 = (f32[64,128]{0,1:T(8,128)S(1)}, f32[64,128]{0,1:T(8,128)S(1)}, u32[]{:S(2)}, u32[]{:S(2)}) collective-permute-start(f32[64,128]{0,1:T(8,128)S(1)} %fusion.36), channel_id=1, source_target_pairs={{15,0},{0,1},{1,2},{2,3},{3,4},{4,5},{5,6},{6,7},{7,8},{8,9},{9,10... | collective-permute-start | bytes 98312 | tf_op jit(solution)/shard_map/ppermute | solution.py:16
  (8 other events, 38.1 us)
where the time goes:
time: 383 us; the launch traced here: 382 us
  waiting for transfers between devices  136 us (36%)
  blocking collectives  111 us (29%)
  other arithmetic  57.7 us (15%)
  starting transfers between devices  41.1 us (11%)
  local copies, waits for them, and re-layouts  31.2 us (8%)
    ppermute x36, waiting for transfers between devices, shifted(): return lax.ppermute(block, axis, route)  136 us
    psum x2, blocking collectives, on_device(): lax.psum((jnp.sum(start * change, axis=1), jnp.sum(change * change, axis=...  73.9 us
    scatter-add x9, other arithmetic, element_images(): return jnp.zeros_like(window).at[:, offsets].add(images)  54.8 us
    ppermute x36, starting transfers between devices, shifted(): return lax.ppermute(block, axis, route)  41.1 us
    psum x1, blocking collectives, on_device(): lax.psum((jnp.sum(right_side * image, axis=1), jnp.sum(image * image, axi...  36.8 us
    gather x18, local copies, waits for them, and re-layouts, element_images(): corners = window[:, offsets]  27.1 us
  transfers between devices with their start and end apart: 36, of which 36 were waited for; matrix products, arithmetic and copies ran while one was open for 0% of the time, Pallas kernels for 0%

commit v1 on v0

--- a/solution.py
+++ b/solution.py
@@ -1,13 +1,20 @@
+import functools
 import math
 
 import jax
 import jax.numpy as jnp
 import numpy as np
 from jax import lax
+from jax.experimental import pallas as pl
+from jax.experimental.pallas import tpu as pltpu
 from jax.sharding import PartitionSpec as P
 
 SWEEPS = 2
 DEGREE = 4
+CX, CY, CZ = 4, 2, 16
+SUB, LANES = 8, 128
+MESH = pl.DeviceIdType.MESH
+HIGHEST = lax.Precision.HIGHEST
 
 
 def shifted(block, axis, distance):
@@ -114,9 +121,355 @@
     return (solution, jnp.stack(history, axis=0))
 
 
+def next_x(plane):
+    return jnp.concatenate([plane[1:], plane[:1]], axis=0)
+
+
+def last_x(plane):
+    return jnp.concatenate([plane[-1:], plane[:-1]], axis=0)
+
+
+def next_z(plane):
+    turned = pltpu.roll(plane, SUB - 1, 1)
+    place = lax.broadcasted_iota(jnp.int32, plane.shape, 1)
+    return jnp.where(place == SUB - 1, pltpu.roll(turned, LANES // 2, 2), turned)
+
+
+def last_z(plane):
+    turned = pltpu.roll(plane, 1, 1)
+    place = lax.broadcasted_iota(jnp.int32, plane.shape, 1)
+    return jnp.where(place == 0, pltpu.roll(turned, LANES // 2, 2), turned)
+
+
+def chebyshev_weights(theta):
+    upper = 1.5 * theta
+    lower = upper / 10.0
+    center = (upper + lower) / 2.0
+    half = (upper - lower) / 2.0
+    sigma = center / half
+    rho_now = 1.0 / sigma
+    direction = [1.0 / center]
+    residual = [jnp.ones_like(theta)]
+    correction = []
+    for step in range(DEGREE):
+        size = len(direction)
+        correction = [
+            direction[k] + correction[k] if k < len(correction) else direction[k]
+            for k in range(size)
+        ]
+        residual = [residual[0]] + [
+            residual[k] - direction[k - 1] if k < len(residual) else -direction[k - 1]
+            for k in range(1, size + 1)
+        ]
+        if step + 1 < DEGREE:
+            rho_next = 1.0 / (2.0 * sigma - rho_now)
+            direction = [
+                rho_next * rho_now * direction[k] + 2.0 * rho_next / half * residual[k]
+                if k < size
+                else 2.0 * rho_next / half * residual[k]
+                for k in range(size + 1)
+            ]
+            rho_now = rho_next
+    return correction, [-value for value in residual[1:]]
+
+
+def kernel(
+    groups, rowcount, total,
+    right_ref, links_ref, coefs_ref, react_ref,
+    out_ref, rms_ref,
+    field, mass, diag, edge_x, edge_y, edge_z, aux,
+    power1, power2, power3, power4, moved, sums,
+    field_send, field_recv, aux_send, aux_recv, moved_send, moved_recv, sums_send, sums_recv,
+):
+    reach = DEGREE // CY
+    grp = lax.axis_index("grp")
+    row = lax.axis_index("row")
+    own = range(reach * CY, reach * CY + CY)
+    nrhs = right_ref.shape[0]
+    count = right_ref.shape[1]
+
+    def row_at(offset):
+        return lax.rem(row + offset + rowcount, rowcount)
+
+    near = [(o, d) for o in sorted(range(-reach, reach + 1), key=lambda o: -abs(o)) for d in range(groups)]
+    near = [(o, d) for o, d in near if o or d]
+
+    barrier = pltpu.get_barrier_semaphore()
+    greeted = 0
+    for o in range(1, rowcount):
+        pl.semaphore_signal(barrier, inc=1, device_id=(grp, row_at(o)), device_id_type=MESH)
+        greeted += 1
+    for o, d in near:
+        if d:
+            peer = (lax.rem(grp + d, groups), row_at(o))
+            pl.semaphore_signal(barrier, inc=1, device_id=peer, device_id_type=MESH)
+            greeted += 1
+
+    home = (grp * rowcount + row) * count
+    slots = jnp.broadcast_to(links_ref[0:1, :] - home, (count, count))
+    slot_of = (slots == lax.broadcasted_iota(jnp.int32, (count, count), 0)).astype(jnp.float32)
+    order = jnp.transpose(slot_of)
+    lanes = lax.broadcasted_iota(jnp.int32, (CX, SUB, LANES), 2)
+    low = lanes < LANES // 2
+    react = jnp.dot(
+        jnp.broadcast_to(react_ref[...], (SUB, count)), slot_of,
+        precision=HIGHEST, preferred_element_type=jnp.float32,
+    )
+    which = lax.broadcasted_iota(jnp.int32, (SUB, count), 0)
+    my_aux = reach * groups + grp
+    aux[my_aux] = jnp.where(
+        which == 0, jnp.broadcast_to(coefs_ref[...], (SUB, count)) * (1.0 / 12.0), react
+    )
+    twice = jnp.concatenate([right_ref[...], right_ref[...]], axis=0)
+    nodes = lax.dot_general(
+        order, twice, (((1,), (1,)), ((), ())), precision=HIGHEST,
+        preferred_element_type=jnp.float32,
+    ).reshape(CX, CY, 2, SUB, LANES)
+    for y in range(CY):
+        field[reach * CY + y, pl.ds(grp * CX, CX)] = jnp.where(low, nodes[:, y, 0], nodes[:, y, 1])
+
+    pl.semaphore_wait(barrier, greeted)
+    aux_copies, field_copies = [], []
+    for k, (o, d) in enumerate(near):
+        peer = (lax.rem(grp + d, groups), row_at(o))
+        copy = pltpu.make_async_remote_copy(
+            src_ref=aux.at[my_aux], dst_ref=aux.at[(reach - o) * groups + grp],
+            send_sem=aux_send.at[k], recv_sem=aux_recv.at[k], device_id=peer, device_id_type=MESH,
+        )
+        copy.start()
+        aux_copies.append(copy)
+    for k, (o, d) in enumerate(near):
+        peer = (lax.rem(grp + d, groups), row_at(o))
+        copy = pltpu.make_async_remote_copy(
+            src_ref=field.at[pl.ds(reach * CY, CY), pl.ds(grp * CX, CX)],
+            dst_ref=field.at[pl.ds((reach - o) * CY, CY), pl.ds(grp * CX, CX)],
+            send_sem=field_send.at[k], recv_sem=field_recv.at[k], device_id=peer, device_id_type=MESH,
+        )
+        copy.start()
+        field_copies.append(copy)
+
+    for copy in aux_copies:
+        copy.wait_recv()
+    blocks = 2 * reach + 1
+    table = aux[...].reshape(blocks * groups * SUB, count)
+    table = jnp.concatenate([table, jnp.zeros((count - table.shape[0], count), jnp.float32)], axis=0)
+    columns = jnp.transpose(table).reshape(CX, CY, 2, SUB, LANES)
+    for b in range(blocks):
+        for g in range(groups):
+            for y in range(CY):
+                for entry, target in ((0, mass), (1, diag)):
+                    at = (b * groups + g) * SUB + entry
+                    first = jnp.broadcast_to(columns[:, y, 0, :, at : at + 1], (CX, SUB, LANES))
+                    second = jnp.broadcast_to(columns[:, y, 1, :, at : at + 1], (CX, SUB, LANES))
+                    target[b * CY + y, g * CX : (g + 1) * CX] = jnp.where(low, first, second)
+    planes = blocks * CY
+    before_xz = before_x = before_z = before = None
+    for y in range(planes - 1):
+        here = mass[y]
+        here_z = here + last_z(here)
+        here_x = here + last_x(here)
+        here_xz = here_z + last_x(here_z)
+        edge_y[y] = here_xz
+        if y:
+            edge_x[y] = here_z + before_z
+            edge_z[y] = here_x + before_x
+            diag[y] = diag[y] + 5.0 * (here_xz + before_xz)
+        before_xz, before_x, before_z = here_xz, here_x, here_z
+
+    def apply_operator(source, target, begin, end):
+        def gathered(y):
+            value = source[y]
+            above = next_z(value)
+            pair = value + above
+            return value, above, pair + next_x(pair)
+
+        last, _, last_sum = gathered(begin - 1)
+        value, above, here_sum = gathered(begin)
+        last_push = mass[begin - 1] * (last_sum + here_sum)
+        for y in range(begin, end):
+            following, following_above, following_sum = gathered(y + 1)
+            push = mass[y] * (here_sum + following_sum)
+            push_y = push + last_push
+            push_x = push_y + last_x(push_y)
+            result = diag[y] * value - push_x + edge_z[y] * above
+            result = result + edge_x[y] * next_x(value) + last_x(edge_x[y] * value)
+            result = result + edge_y[y] * following + edge_y[y - 1] * last
+            target[y] = result + last_z(edge_z[y] * value - push_x)
+            last, last_push = value, push
+            value, above, here_sum = following, following_above, following_sum
+
+    def across(products):
+        return jnp.sum(jnp.sum(products, axis=0), axis=0, keepdims=True)
+
+    def start_sum(number, rows):
+        rows = rows + [jnp.zeros_like(rows[0])] * (sums.shape[2] - len(rows))
+        sums[number, row] = jnp.concatenate(rows, axis=0)
+        copies = []
+        for o in range(1, rowcount):
+            copy = pltpu.make_async_remote_copy(
+                src_ref=sums.at[number, row], dst_ref=sums.at[number, row],
+                send_sem=sums_send.at[number, o - 1], recv_sem=sums_recv.at[number, o - 1],
+                device_id=(grp, row_at(o)), device_id_type=MESH,
+            )
+            copy.start()
+            copies.append(copy)
+        return copies
+
+    def end_sum(number, copies):
+        for copy in copies:
+            copy.wait_recv()
+        added = jnp.sum(sums[number], axis=0)
+        return added + pltpu.roll(added, LANES // 2, 1)
+
+    def spread(line):
+        return jnp.broadcast_to(line, (SUB, LANES))
+
+    def combined(weights, powers, y):
+        value = weights[0] * powers[0][y]
+        for weight, power in zip(weights[1:], powers[1:]):
+            value = value + weight * power[y]
+        return value
+
+    for copy in field_copies:
+        copy.wait_recv()
+    first, final = reach * CY, reach * CY + CY
+    apply_operator(field, power1, first, final)
+    cross = sum(across(field[y] * power1[y]) for y in own)
+    square = sum(across(power1[y] * power1[y]) for y in own)
+    begin = sum(across(field[y] * field[y]) for y in own)
+    bound = start_sum(0, [cross, square, begin])
+    apply_operator(field, power1, 1, first)
+    apply_operator(field, power1, final, planes - 1)
+    apply_operator(power1, power2, 2, planes - 2)
+    apply_operator(power2, power3, 3, planes - 3)
+    apply_operator(power3, power4, 4, planes - 4)
+    powers = [field, power1, power2, power3, power4]
+    added = end_sum(0, bound)
+    correct, differ = chebyshev_weights(spread(added[1:2] / added[0:1]))
+    begin = spread(added[2:3])
+
+    for y in own:
+        moved[y] = combined(differ, powers[1:], y)
+    moved_copies = []
+    for k, o in enumerate(o for o in range(-reach, reach + 1) if o):
+        copy = pltpu.make_async_remote_copy(
+            src_ref=moved.at[pl.ds(reach * CY, CY)], dst_ref=moved.at[pl.ds((reach - o) * CY, CY)],
+            send_sem=moved_send.at[k], recv_sem=moved_recv.at[k],
+            device_id=(grp, row_at(o)), device_id_type=MESH,
+        )
+        copy.start()
+        moved_copies.append(copy)
+    along = sum(across(field[y] * moved[y]) for y in own)
+    length = sum(across(moved[y] * moved[y]) for y in own)
+    step_sum = start_sum(1, [along, length])
+
+    half_rows = [order.reshape(CX, CY, 2, SUB, count)[:, :, z] for z in range(2)]
+    half_rows = [
+        jnp.concatenate([part[:, y].reshape(CX * SUB, count) for y in range(CY)], axis=0)
+        for part in half_rows
+    ]
+
+    def mine(y, value):
+        return jnp.where(grp == 0, value[:CX], value[CX:])
+
+    def to_slots(parts):
+        stacked = jnp.concatenate([part.reshape(CX * SUB, LANES) for part in parts], axis=0)
+        turned = jnp.transpose(stacked)
+        return sum(
+            jnp.dot(
+                turned[z * nrhs : (z + 1) * nrhs], half_rows[z],
+                precision=HIGHEST, preferred_element_type=jnp.float32,
+            )
+            for z in range(2)
+        )
+
+    corrections = [mine(y, combined(correct, powers[:-1], y)) for y in own]
+
+    def rms(omega, along, length, begin):
+        squares = begin - 2.0 * omega * along + omega * omega * length
+        return jnp.sqrt(squares / total)
+
+    added = end_sum(1, step_sum)
+    along, length = spread(added[0:1]), spread(added[1:2])
+    omega = along / length
+    first_rms = rms(omega, along, length, begin)
+    corrections = [omega * part for part in corrections]
+    for copy in moved_copies:
+        copy.wait_recv()
+    for copy in field_copies:
+        copy.wait_send()
+    for y in range(planes):
+        field[y] = field[y] - omega * moved[y]
+    apply_operator(field, power1, 1, planes - 1)
+    apply_operator(power1, power2, 2, planes - 2)
+    apply_operator(power2, power3, 3, planes - 3)
+    apply_operator(power3, power4, 4, planes - 4)
+    along = length = begin = 0.0
+    for y in own:
+        change = combined(differ, powers[1:], y)
+        along = along + across(field[y] * change)
+        length = length + across(change * change)
+        begin = begin + across(field[y] * field[y])
+    step_sum = start_sum(2, [along, length, begin])
+    settled = to_slots(corrections)
+    later = to_slots([mine(y, combined(correct, powers[:-1], y)) for y in own])
+    added = end_sum(2, step_sum)
+    along, length, begin = (spread(added[k : k + 1]) for k in range(3))
+    omega = along / length
+    second_rms = rms(omega, along, length, begin)
+    rms_ref[...] = jnp.concatenate([first_rms[0:1, :nrhs], second_rms[0:1, :nrhs]], axis=0)
+    column = jnp.transpose(jnp.broadcast_to(omega[0:1], (LANES, LANES)))[:nrhs]
+    out_ref[...] = settled + column * later
+    for copy in aux_copies + moved_copies + bound:
+        copy.wait_send()
+    for o in range(1, rowcount):
+        for number in range(1, 3):
+            pltpu.make_async_remote_copy(
+                src_ref=sums.at[number, row], dst_ref=sums.at[number, row],
+                send_sem=sums_send.at[number, o - 1], recv_sem=sums_recv.at[number, o - 1],
+                device_id=(grp, row_at(o)), device_id_type=MESH,
+            ).wait_send()
+
+
+def whole_sweeps(groups, rowcount, right_side, links, coefs, reaction):
+    nrhs, count = right_side.shape
+    reach = DEGREE // CY
+    planes = (2 * reach + 1) * CY
+    window = pltpu.VMEM((planes, groups * CX, SUB, LANES), jnp.float32)
+    nears = groups * (2 * reach + 1) - 1
+    dma = pltpu.SemaphoreType.DMA
+    vmem = pl.BlockSpec(memory_space=pltpu.VMEM)
+    return pl.pallas_call(
+        functools.partial(kernel, groups, rowcount, count * groups * rowcount),
+        out_shape=(
+            jax.ShapeDtypeStruct((nrhs, count), jnp.float32),
+            jax.ShapeDtypeStruct((SWEEPS, nrhs), jnp.float32),
+        ),
+        in_specs=[vmem] * 4,
+        out_specs=(vmem, vmem),
+        scratch_shapes=[
+            window, window, window, window, window, window,
+            pltpu.VMEM(((2 * reach + 1) * groups, SUB, count), jnp.float32),
+            window, window, window, window, window,
+            pltpu.VMEM((3, rowcount, 4, LANES), jnp.float32),
+            dma((nears,)), dma((nears,)), dma((nears,)), dma((nears,)),
+            dma((2 * reach,)), dma((2 * reach,)),
+            dma((3, rowcount - 1)), dma((3, rowcount - 1)),
+        ],
+        compiler_params=pltpu.CompilerParams(collective_id=0, has_side_effects=True),
+    )(right_side, links, coefs.reshape(1, count), reaction.reshape(1, count))
+
+
+def in_one_kernel(mesh):
+    return mesh.shape["grp"] == 2 and mesh.shape["row"] >= 2 * (DEGREE // CY) + 1
+
+
 def solution(mesh):
+    body = on_device
+    if in_one_kernel(mesh):
+        body = functools.partial(whole_sweeps, mesh.shape["grp"], mesh.shape["row"])
     return jax.shard_map(
-        on_device,
+        body,
         mesh=mesh,
         in_specs=(
             P(None, ("grp", "row")),

time: 383 us -> 35.3 us (0.09)
  waiting for transfers between devices: 136 us -> 0 us
  blocking collectives: 111 us -> 0 us
  other arithmetic: 57.7 us -> 0 us
  starting transfers between devices: 41.1 us -> 0 us
  Pallas kernels: 0 us -> 32.5 us
  local copies, waits for them, and re-layouts: 31.2 us -> 1.94 us
    ppermute x36 -> x0, waiting for transfers between devices: 136 us -> none  [shifted(): return lax.ppermute(block, axis, route)]
    psum x3 -> x0, blocking collectives: 111 us -> none  [the longest x2 73.9 us: on_device(): lax.psum((jnp.sum(start * change, axis=1), jnp.sum(change * change, axis=...]
    scatter-add x9 -> x0, other arithmetic: 54.8 us -> none  [element_images(): return jnp.zeros_like(window).at[:, offsets].add(images)]
    ppermute x36 -> x0, starting transfers between devices: 41.1 us -> none  [shifted(): return lax.ppermute(block, axis, route)]
    pallas_call x0 -> x1, Pallas kernels: none -> 32.5 us  [whole_sweeps(): pl.pallas_call(functools.partial(kernel, groups, rowcount, count * groups...]
    gather x18 -> x0, local copies, waits for them, and re-layouts: 27.1 us -> none  [element_images(): corners = window[:, offsets]]
  transfers between devices with their start and end apart: 36 -> 0, of which waited for: 36 -> 0; matrix products, arithmetic and copies ran while one was open for 0% -> 0% of each run, Pallas kernels for 0% -> 0%
where the time goes in v1:
time: 35.3 us; the launch traced here: 35.1 us
  Pallas kernels  32.5 us (92%)
  local copies, waits for them, and re-layouts  1.94 us (5%)
  between operations  0.65 us (2%)
    pallas_call x1, Pallas kernels, whole_sweeps(): pl.pallas_call(functools.partial(kernel, groups, rowcount, count * groups...  32.5 us
    unnamed x4, local copies, waits for them, and re-layouts  1.94 us

profile of v1, /device:TPU:0, one launch (start us, length us, event | category | flops | bytes accessed | tf_op | source)
XLA Modules:
  0.0 35.1 jit_solution(9887340258901880583)
XLA Ops:
  0.6 32.5 %shard_map.59 = (f32[64,128]{1,0:T(8,128)}, f32[2,64]{1,0:T(2,128)}) custom-call(f32[64,128]{1,0:T(8,128)} %right_ref.1, s32[8,128]{1,0:T(8,128)} %links_ref.1, f32[1,128]{1,0:T(1,128)} %bitcast.2, f32[1,128]{1,0:T(1,128)} %bitcast.3), custom_call_target="tpu_custom_call" | custom-call | tf_op jit(solution)/shard_map/pallas_call | solution.py:442
  33.1 0.0 copy-start
  33.1 1.4 %copy.8 = f32[64,128]{1,0:T(8,128)} copy(f32[64,128]{1,0:T(8,128)} %get-tuple-element.4) | data formatting | bytes 65536
  34.5 0.0 copy-done
  34.5 0.6 %copy.9 = f32[2,64]{1,0:T(2,128)} copy(f32[2,64]{1,0:T(2,128)S(1)} %copy-done) | data formatting | bytes 1024
Async XLA Ops:
  33.1 1.4 %copy-start = (f32[2,64]{1,0:T(2,128)S(1)}, f32[2,64]{1,0:T(2,128)}, u32[]{:S(2)}) copy-start(f32[2,64]{1,0:T(2,128)} %get-tuple-element.5) | copy-start | bytes 1540

commit v2 on v1

--- a/solution.py
+++ b/solution.py
@@ -176,7 +176,7 @@
 def kernel(
     groups, rowcount, total,
     right_ref, links_ref, coefs_ref, react_ref,
-    out_ref, rms_ref,
+    packed_ref,
     field, mass, diag, edge_x, edge_y, edge_z, aux,
     power1, power2, power3, power4, moved, sums,
     field_send, field_recv, aux_send, aux_recv, moved_send, moved_recv, sums_send, sums_recv,
@@ -305,7 +305,7 @@
         rows = rows + [jnp.zeros_like(rows[0])] * (sums.shape[2] - len(rows))
         sums[number, row] = jnp.concatenate(rows, axis=0)
         copies = []
-        for o in range(1, rowcount):
+        for o in sorted(range(1, rowcount), key=lambda o: -min(o, rowcount - o)):
             copy = pltpu.make_async_remote_copy(
                 src_ref=sums.at[number, row], dst_ref=sums.at[number, row],
                 send_sem=sums_send.at[number, o - 1], recv_sem=sums_recv.at[number, o - 1],
@@ -417,9 +417,11 @@
     along, length, begin = (spread(added[k : k + 1]) for k in range(3))
     omega = along / length
     second_rms = rms(omega, along, length, begin)
-    rms_ref[...] = jnp.concatenate([first_rms[0:1, :nrhs], second_rms[0:1, :nrhs]], axis=0)
+    packed_ref[pl.ds(nrhs, SUB)] = jnp.where(
+        lax.broadcasted_iota(jnp.int32, (SUB, LANES), 0) == 0, first_rms, second_rms
+    )
     column = jnp.transpose(jnp.broadcast_to(omega[0:1], (LANES, LANES)))[:nrhs]
-    out_ref[...] = settled + column * later
+    packed_ref[pl.ds(0, nrhs)] = settled + column * later
     for copy in aux_copies + moved_copies + bound:
         copy.wait_send()
     for o in range(1, rowcount):
@@ -431,6 +433,12 @@
             ).wait_send()
 
 
+def unpack(packed_ref, out_ref, rms_ref):
+    nrhs = out_ref.shape[0]
+    out_ref[...] = packed_ref[:nrhs]
+    rms_ref[...] = packed_ref[nrhs : nrhs + SWEEPS, :nrhs]
+
+
 def whole_sweeps(groups, rowcount, right_side, links, coefs, reaction):
     nrhs, count = right_side.shape
     reach = DEGREE // CY
@@ -439,14 +447,11 @@
     nears = groups * (2 * reach + 1) - 1
     dma = pltpu.SemaphoreType.DMA
     vmem = pl.BlockSpec(memory_space=pltpu.VMEM)
-    return pl.pallas_call(
+    packed = pl.pallas_call(
         functools.partial(kernel, groups, rowcount, count * groups * rowcount),
-        out_shape=(
-            jax.ShapeDtypeStruct((nrhs, count), jnp.float32),
-            jax.ShapeDtypeStruct((SWEEPS, nrhs), jnp.float32),
-        ),
+        out_shape=jax.ShapeDtypeStruct((nrhs + SUB, count), jnp.float32),
         in_specs=[vmem] * 4,
-        out_specs=(vmem, vmem),
+        out_specs=vmem,
         scratch_shapes=[
             window, window, window, window, window, window,
             pltpu.VMEM(((2 * reach + 1) * groups, SUB, count), jnp.float32),
@@ -458,6 +463,15 @@
         ],
         compiler_params=pltpu.CompilerParams(collective_id=0, has_side_effects=True),
     )(right_side, links, coefs.reshape(1, count), reaction.reshape(1, count))
+    return pl.pallas_call(
+        unpack,
+        out_shape=(
+            jax.ShapeDtypeStruct((nrhs, count), jnp.float32),
+            jax.ShapeDtypeStruct((SWEEPS, nrhs), jnp.float32),
+        ),
+        in_specs=[vmem],
+        out_specs=(vmem, vmem),
+    )(packed)
 
 
 def in_one_kernel(mesh):

time: 35.3 us -> 34.8 us (0.986)
  local copies, waits for them, and re-layouts: 1.94 us -> 0 us
  Pallas kernels: 32.5 us -> 33.9 us
    unnamed x4 -> x0, local copies, waits for them, and re-layouts: 1.94 us -> none
    pallas_call x0 -> x1, Pallas kernels: none -> 1.39 us  [whole_sweeps(): pl.pallas_call(unpack, out_shape=(jax.ShapeDtypeStruct((nrhs, count), jnp...]
where the time goes in v2:
time: 34.8 us; the launch traced here: 34.6 us
  Pallas kernels  33.9 us (97%)
  between operations  0.64 us (2%)
    pallas_call x1, Pallas kernels, whole_sweeps(): pl.pallas_call(functools.partial(kernel, groups, rowcount, count * groups...  32.5 us
    pallas_call x1, Pallas kernels, whole_sweeps(): pl.pallas_call(unpack, out_shape=(jax.ShapeDtypeStruct((nrhs, count), jnp...  1.39 us

profile of v2, /device:TPU:0, one launch (start us, length us, event | category | flops | bytes accessed | tf_op | source)
XLA Modules:
  0.0 34.6 jit_solution(6604842003318175371)
XLA Ops:
  0.6 32.5 %shard_map.59.packed_ref = f32[72,128]{1,0:T(8,128)} custom-call(f32[64,128]{1,0:T(8,128)} %right_ref.1, s32[8,128]{1,0:T(8,128)} %links_ref.1, f32[1,128]{1,0:T(1,128)} %bitcast.2, f32[1,128]{1,0:T(1,128)} %bitcast.3), custom_call_target="tpu_custom_call" | custom-call | tf_op jit(solution)/shard_map/pallas_call | solution.py:450
  33.2 1.4 %shard_map.60 = (f32[64,128]{1,0:T(8,128)}, f32[2,64]{1,0:T(2,128)}) custom-call(f32[72,128]{1,0:T(8,128)} %shard_map.59.packed_ref), custom_call_target="tpu_custom_call" | custom-call | tf_op jit(solution)/shard_map/pallas_call | solution.py:466

commit v3 on v2

--- a/solution.py
+++ b/solution.py
@@ -141,6 +141,34 @@
     return jnp.where(place == 0, pltpu.roll(turned, LANES // 2, 2), turned)
 
 
+def two_sum(a, b):
+    total = a + b
+    part = total - a
+    return total, (a - (total - part)) + (b - part)
+
+
+def halves(a):
+    scaled = 4097.0 * a
+    high = scaled - (scaled - a)
+    return high, a - high
+
+
+def scaled_sum(weights, pairs):
+    total = rest = None
+    for weight, (value, error) in zip(weights, pairs):
+        product = weight * value
+        weight_high, weight_low = halves(weight)
+        high, low = halves(value)
+        lost = ((weight_high * high - product) + weight_high * low + weight_low * high) + weight_low * low
+        lost = lost + weight * error
+        if total is None:
+            total, rest = product, lost
+        else:
+            total, error = two_sum(total, product)
+            rest = rest + (error + lost)
+    return total, rest
+
+
 def chebyshev_weights(theta):
     upper = 1.5 * theta
     lower = upper / 10.0
@@ -178,10 +206,11 @@
     right_ref, links_ref, coefs_ref, react_ref,
     packed_ref,
     field, mass, diag, edge_x, edge_y, edge_z, aux,
-    power1, power2, power3, power4, moved, sums,
-    field_send, field_recv, aux_send, aux_recv, moved_send, moved_recv, sums_send, sums_recv,
+    power1, power2, power3, power4, grams, sums,
+    field_send, field_recv, aux_send, aux_recv, sums_send, sums_recv,
 ):
-    reach = DEGREE // CY
+    half_reach = DEGREE // CY
+    reach = SWEEPS * half_reach
     grp = lax.axis_index("grp")
     row = lax.axis_index("row")
     own = range(reach * CY, reach * CY + CY)
@@ -191,7 +220,8 @@
     def row_at(offset):
         return lax.rem(row + offset + rowcount, rowcount)
 
-    near = [(o, d) for o in sorted(range(-reach, reach + 1), key=lambda o: -abs(o)) for d in range(groups)]
+    far = sorted(range(-reach, reach + 1), key=lambda o: (abs(o) > half_reach, -abs(o)))
+    near = [(o, d) for o in far for d in range(groups)]
     near = [(o, d) for o, d in near if o or d]
 
     barrier = pltpu.get_barrier_semaphore()
@@ -248,33 +278,48 @@
         copy.start()
         field_copies.append(copy)
 
-    for copy in aux_copies:
-        copy.wait_recv()
     blocks = 2 * reach + 1
-    table = aux[...].reshape(blocks * groups * SUB, count)
-    table = jnp.concatenate([table, jnp.zeros((count - table.shape[0], count), jnp.float32)], axis=0)
-    columns = jnp.transpose(table).reshape(CX, CY, 2, SUB, LANES)
-    for b in range(blocks):
-        for g in range(groups):
-            for y in range(CY):
-                for entry, target in ((0, mass), (1, diag)):
-                    at = (b * groups + g) * SUB + entry
-                    first = jnp.broadcast_to(columns[:, y, 0, :, at : at + 1], (CX, SUB, LANES))
-                    second = jnp.broadcast_to(columns[:, y, 1, :, at : at + 1], (CX, SUB, LANES))
-                    target[b * CY + y, g * CX : (g + 1) * CX] = jnp.where(low, first, second)
     planes = blocks * CY
-    before_xz = before_x = before_z = before = None
-    for y in range(planes - 1):
-        here = mass[y]
-        here_z = here + last_z(here)
-        here_x = here + last_x(here)
-        here_xz = here_z + last_x(here_z)
-        edge_y[y] = here_xz
-        if y:
-            edge_x[y] = here_z + before_z
-            edge_z[y] = here_x + before_x
-            diag[y] = diag[y] + 5.0 * (here_xz + before_xz)
-        before_xz, before_x, before_z = here_xz, here_x, here_z
+    inner = [abs(o) <= half_reach for o, d in near]
+    low_plane, top_plane = half_reach * CY, planes - half_reach * CY
+
+    def expand(begin, end):
+        table = aux[begin * groups : end * groups].reshape((end - begin) * groups * SUB, count)
+        spare = -table.shape[0] % count
+        table = jnp.concatenate([table, jnp.zeros((spare, count), jnp.float32)], axis=0)
+        columns = [
+            jnp.transpose(table[k : k + count]).reshape(CX, CY, 2, SUB, LANES)
+            for k in range(0, table.shape[0], count)
+        ]
+        for b in range(begin, end):
+            for g in range(groups):
+                for y in range(CY):
+                    for entry, target in ((0, mass), (1, diag)):
+                        part, at = divmod(((b - begin) * groups + g) * SUB + entry, count)
+                        part = columns[part]
+                        first = jnp.broadcast_to(part[:, y, 0, :, at : at + 1], (CX, SUB, LANES))
+                        second = jnp.broadcast_to(part[:, y, 1, :, at : at + 1], (CX, SUB, LANES))
+                        target[b * CY + y, g * CX : (g + 1) * CX] = jnp.where(low, first, second)
+
+    def edges(begin, end):
+        before_xz = before_x = before_z = None
+        for y in range(begin, end):
+            here = mass[y]
+            here_z = here + last_z(here)
+            here_x = here + last_x(here)
+            here_xz = here_z + last_x(here_z)
+            edge_y[y] = here_xz
+            if y > begin:
+                edge_x[y] = here_z + before_z
+                edge_z[y] = here_x + before_x
+                diag[y] = diag[y] + 5.0 * (here_xz + before_xz)
+            before_xz, before_x, before_z = here_xz, here_x, here_z
+
+    for copy, is_inner in zip(aux_copies, inner):
+        if is_inner:
+            copy.wait_recv()
+    expand(half_reach, blocks - half_reach)
+    edges(low_plane, top_plane - 1)
 
     def apply_operator(source, target, begin, end):
         def gathered(y):
@@ -301,13 +346,13 @@
     def across(products):
         return jnp.sum(jnp.sum(products, axis=0), axis=0, keepdims=True)
 
-    def start_sum(number, rows):
-        rows = rows + [jnp.zeros_like(rows[0])] * (sums.shape[2] - len(rows))
-        sums[number, row] = jnp.concatenate(rows, axis=0)
+    def start_sum(number, slots, rows):
+        rows = rows + [jnp.zeros_like(rows[0])] * (slots.shape[1] - len(rows))
+        slots[row] = jnp.concatenate(rows, axis=0)
         copies = []
         for o in sorted(range(1, rowcount), key=lambda o: -min(o, rowcount - o)):
             copy = pltpu.make_async_remote_copy(
-                src_ref=sums.at[number, row], dst_ref=sums.at[number, row],
+                src_ref=slots.at[row], dst_ref=slots.at[row],
                 send_sem=sums_send.at[number, o - 1], recv_sem=sums_recv.at[number, o - 1],
                 device_id=(grp, row_at(o)), device_id_type=MESH,
             )
@@ -315,11 +360,15 @@
             copies.append(copy)
         return copies
 
-    def end_sum(number, copies):
+    def end_sum(slots, copies):
         for copy in copies:
             copy.wait_recv()
-        added = jnp.sum(sums[number], axis=0)
-        return added + pltpu.roll(added, LANES // 2, 1)
+        added, rest = slots[0], jnp.zeros_like(slots[0])
+        for k in range(1, rowcount):
+            added, error = two_sum(added, slots[k])
+            rest = rest + error
+        added, error = two_sum(added, pltpu.roll(added, LANES // 2, 1))
+        return added, rest + pltpu.roll(rest, LANES // 2, 1) + error
 
     def spread(line):
         return jnp.broadcast_to(line, (SUB, LANES))
@@ -330,38 +379,30 @@
             value = value + weight * power[y]
         return value
 
-    for copy in field_copies:
-        copy.wait_recv()
-    first, final = reach * CY, reach * CY + CY
-    apply_operator(field, power1, first, final)
-    cross = sum(across(field[y] * power1[y]) for y in own)
-    square = sum(across(power1[y] * power1[y]) for y in own)
-    begin = sum(across(field[y] * field[y]) for y in own)
-    bound = start_sum(0, [cross, square, begin])
-    apply_operator(field, power1, 1, first)
-    apply_operator(field, power1, final, planes - 1)
-    apply_operator(power1, power2, 2, planes - 2)
-    apply_operator(power2, power3, 3, planes - 3)
-    apply_operator(power3, power4, 4, planes - 4)
+    for copy, is_inner in zip(field_copies, inner):
+        if is_inner:
+            copy.wait_recv()
     powers = [field, power1, power2, power3, power4]
-    added = end_sum(0, bound)
-    correct, differ = chebyshev_weights(spread(added[1:2] / added[0:1]))
-    begin = spread(added[2:3])
-
-    for y in own:
-        moved[y] = combined(differ, powers[1:], y)
-    moved_copies = []
-    for k, o in enumerate(o for o in range(-reach, reach + 1) if o):
-        copy = pltpu.make_async_remote_copy(
-            src_ref=moved.at[pl.ds(reach * CY, CY)], dst_ref=moved.at[pl.ds((reach - o) * CY, CY)],
-            send_sem=moved_send.at[k], recv_sem=moved_recv.at[k],
-            device_id=(grp, row_at(o)), device_id_type=MESH,
-        )
-        copy.start()
-        moved_copies.append(copy)
-    along = sum(across(field[y] * moved[y]) for y in own)
-    length = sum(across(moved[y] * moved[y]) for y in own)
-    step_sum = start_sum(1, [along, length])
+    for k in range(DEGREE):
+        apply_operator(powers[k], powers[k + 1], low_plane + k + 1, top_plane - k - 1)
+    pairs = [(j, k) for j in range(DEGREE + 1) for k in range(max(j, 1), DEGREE + 1)]
+    products = [
+        across(sum(powers[j][y] * powers[k][y] for y in own)) for j, k in pairs
+    ]
+    bound = start_sum(0, grams, products)
+    for copy, is_inner in zip(aux_copies, inner):
+        if not is_inner:
+            copy.wait_recv()
+    expand(0, half_reach)
+    expand(blocks - half_reach, blocks)
+    edges(0, low_plane + 1)
+    edges(top_plane - 2, planes - 1)
+    for copy, is_inner in zip(field_copies, inner):
+        if not is_inner:
+            copy.wait_recv()
+    for k in range(DEGREE):
+        apply_operator(powers[k], powers[k + 1], k + 1, low_plane + k + 1)
+        apply_operator(powers[k], powers[k + 1], top_plane - k - 1, planes - k - 1)
 
     half_rows = [order.reshape(CX, CY, 2, SUB, count)[:, :, z] for z in range(2)]
     half_rows = [
@@ -383,54 +424,49 @@
             for z in range(2)
         )
 
-    corrections = [mine(y, combined(correct, powers[:-1], y)) for y in own]
-
-    def rms(omega, along, length, begin):
-        squares = begin - 2.0 * omega * along + omega * omega * length
-        return jnp.sqrt(squares / total)
-
-    added = end_sum(1, step_sum)
-    along, length = spread(added[0:1]), spread(added[1:2])
-    omega = along / length
-    first_rms = rms(omega, along, length, begin)
-    corrections = [omega * part for part in corrections]
-    for copy in moved_copies:
-        copy.wait_recv()
+    added, rest = end_sum(grams, bound)
+    gram = {
+        pair: (spread(added[at : at + 1]), spread(rest[at : at + 1])) for at, pair in enumerate(pairs)
+    }
+    correct, differ = chebyshev_weights(gram[1, 1][0] / gram[0, 1][0])
+    along = scaled_sum(differ, [gram[0, k] for k in range(1, DEGREE + 1)])
+    length = scaled_sum(
+        differ,
+        [
+            scaled_sum(differ, [gram[min(j, k), max(j, k)] for k in range(1, DEGREE + 1)])
+            for j in range(1, DEGREE + 1)
+        ],
+    )
+    omega = (along[0] + along[1]) / (length[0] + length[1])
+    corrections = [omega * mine(y, combined(correct, powers[:-1], y)) for y in own]
     for copy in field_copies:
         copy.wait_send()
-    for y in range(planes):
-        field[y] = field[y] - omega * moved[y]
-    apply_operator(field, power1, 1, planes - 1)
-    apply_operator(power1, power2, 2, planes - 2)
-    apply_operator(power2, power3, 3, planes - 3)
-    apply_operator(power3, power4, 4, planes - 4)
+    steps = [omega * weight for weight in differ]
+    for y in range(low_plane, top_plane):
+        field[y] = field[y] - combined(steps, powers[1:], y)
+    for k in range(DEGREE):
+        apply_operator(powers[k], powers[k + 1], low_plane + k + 1, top_plane - k - 1)
     along = length = begin = 0.0
     for y in own:
         change = combined(differ, powers[1:], y)
         along = along + across(field[y] * change)
         length = length + across(change * change)
         begin = begin + across(field[y] * field[y])
-    step_sum = start_sum(2, [along, length, begin])
+    step_sum = start_sum(1, sums, [along, length, begin])
     settled = to_slots(corrections)
     later = to_slots([mine(y, combined(correct, powers[:-1], y)) for y in own])
-    added = end_sum(2, step_sum)
+    added = sum(end_sum(sums, step_sum))
     along, length, begin = (spread(added[k : k + 1]) for k in range(3))
     omega = along / length
-    second_rms = rms(omega, along, length, begin)
+    first_rms = jnp.sqrt(begin / total)
+    second_rms = jnp.sqrt((begin - 2.0 * omega * along + omega * omega * length) / total)
     packed_ref[pl.ds(nrhs, SUB)] = jnp.where(
         lax.broadcasted_iota(jnp.int32, (SUB, LANES), 0) == 0, first_rms, second_rms
     )
     column = jnp.transpose(jnp.broadcast_to(omega[0:1], (LANES, LANES)))[:nrhs]
     packed_ref[pl.ds(0, nrhs)] = settled + column * later
-    for copy in aux_copies + moved_copies + bound:
+    for copy in aux_copies + bound + step_sum:
         copy.wait_send()
-    for o in range(1, rowcount):
-        for number in range(1, 3):
-            pltpu.make_async_remote_copy(
-                src_ref=sums.at[number, row], dst_ref=sums.at[number, row],
-                send_sem=sums_send.at[number, o - 1], recv_sem=sums_recv.at[number, o - 1],
-                device_id=(grp, row_at(o)), device_id_type=MESH,
-            ).wait_send()
 
 
 def unpack(packed_ref, out_ref, rms_ref):
@@ -441,7 +477,7 @@
 
 def whole_sweeps(groups, rowcount, right_side, links, coefs, reaction):
     nrhs, count = right_side.shape
-    reach = DEGREE // CY
+    reach = SWEEPS * (DEGREE // CY)
     planes = (2 * reach + 1) * CY
     window = pltpu.VMEM((planes, groups * CX, SUB, LANES), jnp.float32)
     nears = groups * (2 * reach + 1) - 1
@@ -455,11 +491,11 @@
         scratch_shapes=[
             window, window, window, window, window, window,
             pltpu.VMEM(((2 * reach + 1) * groups, SUB, count), jnp.float32),
-            window, window, window, window, window,
-            pltpu.VMEM((3, rowcount, 4, LANES), jnp.float32),
+            window, window, window, window,
+            pltpu.VMEM((rowcount, 2 * SUB, LANES), jnp.float32),
+            pltpu.VMEM((rowcount, 4, LANES), jnp.float32),
             dma((nears,)), dma((nears,)), dma((nears,)), dma((nears,)),
-            dma((2 * reach,)), dma((2 * reach,)),
-            dma((3, rowcount - 1)), dma((3, rowcount - 1)),
+            dma((SWEEPS, rowcount - 1)), dma((SWEEPS, rowcount - 1)),
         ],
         compiler_params=pltpu.CompilerParams(collective_id=0, has_side_effects=True),
     )(right_side, links, coefs.reshape(1, count), reaction.reshape(1, count))
@@ -475,7 +511,7 @@
 
 
 def in_one_kernel(mesh):
-    return mesh.shape["grp"] == 2 and mesh.shape["row"] >= 2 * (DEGREE // CY) + 1
+    return mesh.shape["grp"] == 2 and mesh.shape["row"] >= 2 * SWEEPS * (DEGREE // CY) + 1
 
 
 def solution(mesh):

time: 34.8 us -> 30.9 us (0.89)
  Pallas kernels: 33.9 us -> 30 us
    pallas_call x1, Pallas kernels: 32.5 us -> 28.6 us  [whole_sweeps(): pl.pallas_call(functools.partial(kernel, groups, rowcount, count * groups...]
where the time goes in v3:
time: 30.9 us; the launch traced here: 30.7 us
  Pallas kernels  30 us (97%)
  between operations  0.64 us (2%)
    pallas_call x1, Pallas kernels, whole_sweeps(): pl.pallas_call(functools.partial(kernel, groups, rowcount, count * groups...  28.6 us
    pallas_call x1, Pallas kernels, whole_sweeps(): pl.pallas_call(unpack, out_shape=(jax.ShapeDtypeStruct((nrhs, count), jnp...  1.39 us

profile of v3, /device:TPU:0, one launch (start us, length us, event | category | flops | bytes accessed | tf_op | source)
XLA Modules:
  0.0 30.7 jit_solution(11320453053888866261)
XLA Ops:
  0.6 28.6 %shard_map.59.packed_ref = f32[72,128]{1,0:T(8,128)} custom-call(f32[64,128]{1,0:T(8,128)} %right_ref.1, s32[8,128]{1,0:T(8,128)} %links_ref.1, f32[1,128]{1,0:T(1,128)} %bitcast.2, f32[1,128]{1,0:T(1,128)} %bitcast.3), custom_call_target="tpu_custom_call" | custom-call | tf_op jit(solution)/shard_map/pallas_call | solution.py:486
  29.3 1.4 %shard_map.60 = (f32[64,128]{1,0:T(8,128)}, f32[2,64]{1,0:T(2,128)}) custom-call(f32[72,128]{1,0:T(8,128)} %shard_map.59.packed_ref), custom_call_target="tpu_custom_call" | custom-call | tf_op jit(solution)/shard_map/pallas_call | solution.py:502
